TPU v7x, 256 devices: a whole 4x4x8 slice. The times are simulated.
256 devices in a mesh: row: 8 (over y, core), col: 32 (over x, z).
Axes of the slice: x: 4, y: 4, z: 8, core: 2. Of those that a mesh axis runs over, the one named last changes fastest.
Arguments:
- adjacency: int32 [16384, 32768], P('row', 'col'), may hold values from 0 to 1, as said below
Outputs:
- closure: bfloat16 [16384, 32768], P('row', 'col')
Inputs may be any that keep to these rules, and one draw needn't show every extreme that they name: `adjacency`: every entry is 0 or 1; there is no bound on the number of ones in a row, a column or a block, and their share differs widely between rows and between columns.
All inputs are finite; a program needn't handle non-finite values.
Results may differ from a plain program's by a relative error of at most 0.001.
Values may be sent and summed in bfloat16 or wider, within the bound.
A program may use at most 192 MiB of HBM per device.

v0:
```python
import jax
import jax.numpy as jnp
from jax import lax
from jax.sharding import PartitionSpec as P

PANEL = 512
PANELS = 4


def from_root(shard, axis, root):
    mine = lax.axis_index(axis) == root
    return lax.psum(jnp.where(mine, shard, jnp.zeros_like(shard)), axis)


def picked(shard, axis, root):
    return lax.dynamic_index_in_dim(lax.all_gather(shard, axis), root, 0, keepdims=False)


def per_device(adjacency):
    block_rows, block_cols = adjacency.shape
    totals = jnp.zeros((block_rows, block_cols), jnp.float32)
    for panel_index in range(PANELS):
        leading = panel_index * PANEL
        col_offset = leading % block_cols
        row_offset = leading % block_rows
        left_panel = adjacency[:, col_offset : col_offset + PANEL].astype(jnp.bfloat16)
        left_panel = from_root(left_panel, "col", leading // block_cols)
        right_panel = adjacency[row_offset : row_offset + PANEL, :].astype(jnp.bfloat16)
        right_panel = picked(right_panel, "row", leading // block_rows)
        totals = totals + jnp.dot(left_panel, right_panel, preferred_element_type=jnp.float32)
    closure = jnp.where(totals > 0.5, 1.0, adjacency.astype(jnp.float32))
    return closure.astype(jnp.bfloat16)


def solution(mesh):
    in_specs = (P("row", "col"),)
    out_specs = P("row", "col")
    return jax.shard_map(
        per_device, mesh=mesh, in_specs=in_specs, out_specs=out_specs, check_vma=False
    )
```

profile of v0, /device:TPU:1, one launch (start us, length us, event | category | flops | bytes accessed | tf_op | source)
XLA Modules:
  0.0 278.8 jit_solution(17709794389929564492)
XLA Ops:
  7.4 0.0 all-reduce.3.cloned.1.call-start
  7.4 6.6 %convert.8 = bf16[2048,1024]{1,0:T(8,128)(2,1)} convert(s32[2048,1024]{1,0:T(8,128)} %param.1) | non-fusion elementwise | flops 2097152 | bytes 12582912 | tf_op jit(solution)/shard_map/convert.5
  14.0 4.9 %broadcast_select_fusion = (bf16[2048,512]{1,0:T(8,128)(2,1)}, bf16[2048,512]{1,0:T(8,128)(2,1)}, bf16[2048,512]{1,0:T(8,128)(2,1)}, bf16[2048,512]{1,0:T(8,128)(2,1)}) fusion(pred[]{:T(512)S(6)} %eq.9, bf16[2048,1024]{1,0:T(8,128)(2,1)} %convert.8, pred[]{:T(512)S(6)} %eq.8), kind=kLoop, calls=%fused_computation.2 | loop fusion | flops 4194304 | bytes 12582914 | tf_op jit(solution)/shard_map/jit(_where)/select_n | solution.py:12
  18.9 0.0 all-reduce.3.cloned.1.call-update
  18.9 0.0 all-gather.11.cloned.1.call-start
  18.9 4.3 %fusion.7 = (bf16[512,1024]{1,0:T(8,128)(2,1)}, bf16[512,1024]{1,0:T(8,128)(2,1)}, bf16[512,1024]{1,0:T(8,128)(2,1)}, bf16[512,1024]{1,0:T(8,128)(2,1)}) fusion(bf16[2048,1024]{1,0:T(8,128)(2,1)} %convert.8), kind=kLoop, calls=%fused_computation.13 | loop fusion | bytes 8388608 | tf_op jit(solution)/shard_map/slice | solution.py:28
  23.2 0.0 all-gather.11.cloned.1.call-update
  23.2 0.0 all-gather.9.cloned.1.call-start
  23.3 0.5 all-gather.9.cloned.1.call-update
  23.8 0.0 all-gather.13.cloned.1.call-start
  23.9 0.5 all-gather.13.cloned.1.call-update
  24.4 0.0 all-gather.15.cloned.1.call-start
  24.5 0.7 all-gather.15.cloned.1.call-update
  25.1 209.5 %all-reduce.3.cloned.1.call-done = (bf16[2048,512]{1,0:T(8,128)(2,1)}, bf16[2048,512]{1,0:T(8,128)(2,1)}, bf16[2048,512]{1,0:T(8,128)(2,1)}, bf16[2048,512]{1,0:T(8,128)(2,1)}) async-done(((bf16[2048,512]{1,0:T(8,128)(2,1)}, bf16[2048,512]{1,0:T(8,128)(2,1)}, bf16[2048,512]{1,0:T(8,128)(2,1)}, bf16[2048,512]{1,0:T(8,128)(2,1)}), (bf16[2048,512]{1,0:T(8,128)(2,1)}, bf16[2048,512]{1,0:T(8,128)(2,1)}, ...) | async-done | bytes 8388624 | tf_op jit(solution)/shard_map/psum | solution.py:12
  234.6 0.0 all-gather.11.cloned.1.call-done
  234.6 0.0 copy-start.1
  234.6 7.6 %fusion.3 = f32[2048,1024]{1,0:T(8,128)} fusion(bf16[2048,512]{1,0:T(8,128)(2,1)} %get-tuple-element.7, bf16[4096,1024]{1,0:T(8,128)(2,1)} %all-gather.11.cloned.1.call-done), kind=kOutput, calls=%fused_computation.9 | convolution fusion | flops 2147483648 | bytes 11534336 | tf_op jit(solution)/shard_map/dot_general | solution.py:30
  242.2 0.0 all-gather.9.cloned.1.call-done
  242.2 0.0 copy-done.1
  242.2 6.8 %fusion.5 = f32[2048,1024]{1,0:T(8,128)} fusion(bf16[2048,512]{1,0:T(8,128)(2,1)S(1)} %copy-done.1, bf16[4096,1024]{1,0:T(8,128)(2,1)} %all-gather.9.cloned.1.call-done), kind=kOutput, calls=%fused_computation.11 | convolution fusion | flops 2147483648 | bytes 11534336 | tf_op jit(solution)/shard_map/dot_general | solution.py:30
  249.0 0.0 all-gather.13.cloned.1.call-done
  249.0 0.0 copy-start
  249.0 7.6 %fusion.1 = f32[2048,1024]{1,0:T(8,128)} fusion(bf16[2048,512]{1,0:T(8,128)(2,1)} %get-tuple-element.5, bf16[4096,1024]{1,0:T(8,128)(2,1)} %all-gather.13.cloned.1.call-done), kind=kOutput, calls=%fused_computation.7 | convolution fusion | flops 2147483648 | bytes 11534336 | tf_op jit(solution)/shard_map/dot_general | solution.py:30
  256.6 0.0 all-gather.15.cloned.1.call-done
  256.6 0.0 copy-done
  256.6 14.6 %select_convert_fusion = bf16[2048,1024]{1,0:T(8,128)(2,1)} fusion(s32[2048,1024]{1,0:T(8,128)} %param.1, f32[2048,1024]{1,0:T(8,128)} %fusion.1, f32[2048,1024]{1,0:T(8,128)} %fusion.5, f32[2048,1024]{1,0:T(8,128)} %fusion.3, bf16[2048,512]{1,0:T(8,128)(2,1)S(1)} %copy-done, bf16[4096,1024]{1,0:T(8,128)(2,1)} %all-gather.15.cloned.1.call-done), kind=kOutput, calls=%fused_computation | convolution fusion | flops 2162163712 | bytes 40894464 | tf_op jit(solution)/shard_map/dot_general | solution.py:30
Async XLA Ops:
  7.4 227.2 %all-reduce.3.cloned.1.call-start = ((), (), s32[]{:S(2)}) async-start(), calls=%async_computation.4 | async-start | bytes 16777216 | tf_op jit(solution)/shard_map/psum | solution.py:12
  18.9 215.7 %all-gather.11.cloned.1.call-start = ((), (), s32[]{:S(2)}) async-start(), calls=%async_computation.1 | async-start | bytes 9437184 | tf_op jit(solution)/shard_map/all_gather | solution.py:16
  23.2 218.9 %all-gather.9.cloned.1.call-start = ((), (), s32[]{:S(2)}) async-start(), calls=%async_computation | async-start | bytes 9437184 | tf_op jit(solution)/shard_map/all_gather | solution.py:16
  23.8 225.1 %all-gather.13.cloned.1.call-start = ((), (), s32[]{:S(2)}) async-start(), calls=%async_computation.2 | async-start | bytes 9437184 | tf_op jit(solution)/shard_map/all_gather | solution.py:16
  24.4 232.2 %all-gather.15.cloned.1.call-start = ((), (), s32[]{:S(2)}) async-start(), calls=%async_computation.3 | async-start | bytes 9437184 | tf_op jit(solution)/shard_map/all_gather | solution.py:16
  234.6 7.6 %copy-start.1 = (bf16[2048,512]{1,0:T(8,128)(2,1)S(1)}, bf16[2048,512]{1,0:T(8,128)(2,1)}, u32[]{:S(2)}) copy-start(bf16[2048,512]{1,0:T(8,128)(2,1)} %get-tuple-element.6) | copy-start | bytes 6291460
  249.0 7.6 %copy-start = (bf16[2048,512]{1,0:T(8,128)(2,1)S(1)}, bf16[2048,512]{1,0:T(8,128)(2,1)}, u32[]{:S(2)}) copy-start(bf16[2048,512]{1,0:T(8,128)(2,1)} %get-tuple-element.8) | copy-start | bytes 6291460
Sparse Core Ops, SparseCore 0:
  19.0 215.5 all-reduce.2
Sparse Core Ops, SparseCore 1:
  23.3 56.3 all-gather.10
  81.4 52.2 all-gather.8
  135.4 52.2 all-gather.12
  189.6 52.2 all-gather.14
where the time goes:
time: 279 us
  waiting for transfers between devices  211 us (76%)
  matrix products  36.6 us (13%)
  between operations  15.1 us (5%)
  other arithmetic  11.5 us (4%)
  local copies, waits for them, and re-layouts  4.28 us (2%)
    psum x1, waiting for transfers between devices, from_root(): return lax.psum(jnp.where(mine, shard, jnp.zeros_like(shard)), axis)  209 us
    dot_general x4, matrix products, per_device(): jnp.dot(left_panel, right_panel, preferred_element_type=jnp.float32)  36.6 us
    another operation x1, other arithmetic  6.64 us
  transfers between devices with their start and end apart: 5, of which 1 were waited for; matrix products, arithmetic and copies ran while one was open for 9% of the time, Pallas kernels for 0%

commit v1 on v0

v1 whole, which is shorter than its diff:
```python
import jax
import jax.numpy as jnp
from jax import lax
from jax.experimental import pallas as pl
from jax.experimental.pallas import tpu as pltpu
from jax.sharding import PartitionSpec as P

MESH = pl.DeviceIdType.MESH
XS, ZS, YS = 4, 8, 4
ROOTS = 2
STEPS = ((0, 1), (0, -1), (1, 0), (-1, 0))
TREES = (
    ".0000000122232031212001113313002",
    ".1111111031120220001130302132333",
    ".3333333200011112120222221221220",
    ".2222222313303303333313030000111",
)
CHUNK = 16
LAG = 2.2
RCHUNK = 64
RLAG = 2
PIECE = 128
BLOCK = 256
FIRST = 26
EVERY = 3


def tables():
    depths, children = [], []
    for tree in TREES:
        parent = {}
        for p, c in enumerate(tree):
            if c != ".":
                dx, dz = STEPS[int(c)]
                parent[p] = ((p // ZS - dx) % XS * ZS + (p % ZS - dz) % ZS, int(c))
        depth = []
        for p in range(XS * ZS):
            d, q = 0, p
            while q in parent:
                d, q = d + 1, parent[q][0]
            depth.append(d)
        depths.append(depth)
        kids = [[0] * (XS * ZS) for _ in range(4)]
        for u, c in parent.values():
            kids[c][u] = 1
        children.append(kids)
    return depths, children


DEPTHS, CHILDREN = tables()
LAGS = [[round(LAG * d) for d in depth] for depth in DEPTHS]
MAX_LAG = max(map(max, LAGS))


def lookup(values, p):
    total = jnp.int32(0)
    for bit in range(max(values).bit_length()):
        mask = sum(((v >> bit) & 1) << i for i, v in enumerate(values))
        mask = mask - (1 << 32) if mask >= 1 << 31 else mask
        total = total + (lax.shift_right_logical(jnp.int32(mask), p) & 1) * (1 << bit)
    return total


def kernel(adj_ref, out_ref, stage, own, left, right, load_sem, recv_sem, send_sem, ring_sem, ring_send, pair_sem, pair_send):
    rows, cols = own.shape
    chunks = rows // (4 * CHUNK)
    half = rows // 2
    rchunks = half // RCHUNK
    pieces = rows // PIECE
    row, col = lax.axis_index("row"), lax.axis_index("col")
    y, core = row // 2, row % 2
    x, z = col // ZS, col % ZS
    towards = [lax.rem(x + dx + XS, XS) * ZS + lax.rem(z + dz + ZS, ZS) for dx, dz in STEPS]
    partner = row + 1 - 2 * core
    up, down = lax.rem(y + 1, YS) * 2 + core, lax.rem(y + YS - 1, YS) * 2 + core

    barrier = pltpu.get_barrier_semaphore()
    for c in towards:
        pl.semaphore_signal(barrier, inc=1, device_id=(row, c), device_id_type=MESH)
    for r in (partner, up, down):
        pl.semaphore_signal(barrier, inc=1, device_id=(r, col), device_id_type=MESH)

    def load(i):
        part = pl.ds(i * PIECE, PIECE)
        return pltpu.make_async_copy(adj_ref.at[part, :], stage.at[part, :], load_sem.at[i])

    def convert(i):
        load(i).wait()
        part = pl.ds(pl.multiple_of(i * PIECE, PIECE), PIECE)
        piece = stage[part, :].astype(jnp.float32).astype(jnp.bfloat16)
        own[part, :] = piece
        for s in range(ROOTS):
            @pl.when(col == s)
            def _():
                left[s, part, :] = piece

        @pl.when(row == 0)
        def _():
            right[part, :] = piece

    for i in range(pieces):
        load(i).start()
    convert(0)

    trees = []
    for s in range(ROOTS):
        p = x * ZS + lax.rem(z - s + ZS, ZS)
        for t in range(4):
            lag = lookup(LAGS[t], p)
            kids = [lookup(CHILDREN[t][d], p) for d in range(4)]
            trees.append((s, t, lag, kids))

    def tree_copy(s, t, k, d):
        part = pl.ds(pl.multiple_of((k * 4 + t) * CHUNK, CHUNK), CHUNK)
        ref = left.at[s, part, :]
        return pltpu.make_async_remote_copy(
            src_ref=ref, dst_ref=ref, send_sem=send_sem.at[s * 4 + t, d], recv_sem=recv_sem.at[s * 4 + t, k],
            device_id=(row, towards[d]), device_id_type=MESH,
        )

    hop = jnp.where(core == 0, y, lax.rem(YS - y, YS))
    onward = jnp.where(core == 0, up, down)

    def ring_part(k, h):
        return right.at[pl.ds(pl.multiple_of((2 * k + h) * RCHUNK, RCHUNK), RCHUNK), :]

    def ring_copy(k, h, device):
        ref = ring_part(k, h)
        return pltpu.make_async_remote_copy(
            src_ref=ref, dst_ref=ref, send_sem=ring_send, recv_sem=ring_sem.at[k], device_id=(device, col), device_id_type=MESH,
        )

    def pair_copy(k, h):
        ref = ring_part(k, h)
        return pltpu.make_async_remote_copy(
            src_ref=ref, dst_ref=ref, send_sem=pair_send, recv_sem=pair_sem, device_id=(partner, col), device_id_type=MESH,
        )

    pl.semaphore_wait(barrier, 7)

    def multiply(b):
        part = pl.ds(pl.multiple_of(b * BLOCK, BLOCK), BLOCK)
        width = 256

        @pl.loop(0, cols // width)
        def _(j):
            span = pl.ds(pl.multiple_of(j * width, width), width)
            counts = jnp.dot(left[0, part, :], right[:half, span], preferred_element_type=jnp.float32)
            counts = counts + jnp.dot(left[1, part, :], right[half:, span], preferred_element_type=jnp.float32)
            out_ref[part, span] = jnp.where(counts > 0.5, 1.0, own[part, span].astype(jnp.float32)).astype(jnp.bfloat16)

    steps = FIRST + EVERY * (rows // BLOCK - 1) + 1

    def step(n, carry):
        k = n - hop * RLAG - core

        @pl.when((k >= 0) & (k < rchunks))
        def _():
            @pl.when(row != 0)
            def _():
                ring_copy(k, core, onward).wait_recv()

            @pl.when(hop < YS - 1)
            def _():
                ring_copy(k, core, onward).start()

            @pl.when(row != 1)
            def _():
                pair_copy(k, core).start()

            @pl.when(row == 0)
            def _():
                ring_copy(k, 1, partner).start()

        for s, t, lag, kids in trees:
            k = n - lag

            @pl.when((k >= 0) & (k < chunks))
            def _(s=s, t=t, k=k, kids=kids):
                @pl.when(col != s)
                def _():
                    tree_copy(s, t, k, 0).wait_recv()

                for d in range(4):
                    if max(CHILDREN[t][d]):
                        @pl.when(kids[d] == 1)
                        def _(d=d):
                            tree_copy(s, t, k, d).start()

        @pl.when(n + 1 < pieces)
        def _():
            convert(n + 1)

        @pl.when(n == FIRST - 1)
        def _():
            @pl.when(row != 0)
            def _():
                ref = right.at[pl.ds(0, half), :]
                pltpu.make_async_remote_copy(
                    src_ref=ref, dst_ref=ref, send_sem=pair_send, recv_sem=pair_sem, device_id=(partner, col),
                    device_id_type=MESH,
                ).wait_recv()

        @pl.when((n >= FIRST) & (lax.rem(n - FIRST + EVERY, EVERY) == 0))
        def _():
            multiply((n - FIRST) // EVERY)

        return carry

    lax.fori_loop(0, steps, step, 0)

    for s, t, lag, kids in trees:
        for d in range(4):
            if max(CHILDREN[t][d]):
                @pl.when(kids[d] == 1)
                def _(s=s, t=t, d=d):
                    ref = left.at[0, pl.ds(0, chunks * CHUNK), :]
                    pltpu.make_async_remote_copy(
                        src_ref=ref, dst_ref=ref, send_sem=send_sem.at[s * 4 + t, d], recv_sem=recv_sem.at[0, 0],
                        device_id=(row, towards[d]), device_id_type=MESH,
                    ).wait_send()

    def drain(sem, other):
        ref = right.at[pl.ds(0, half), :]
        pltpu.make_async_remote_copy(
            src_ref=ref, dst_ref=ref, send_sem=sem, recv_sem=ring_sem.at[0], device_id=(other, col), device_id_type=MESH,
        ).wait_send()

    @pl.when(hop < YS - 1)
    def _():
        drain(ring_send, onward)

    @pl.when(row == 0)
    def _():
        drain(ring_send, partner)

    @pl.when(row != 1)
    def _():
        drain(pair_send, partner)


def per_device(adjacency):
    rows, cols = adjacency.shape
    chunks = rows // (4 * CHUNK)
    return pl.pallas_call(
        kernel,
        name="closure",
        out_shape=jax.ShapeDtypeStruct((rows, cols), jnp.bfloat16),
        in_specs=[pl.BlockSpec(memory_space=pl.ANY)],
        out_specs=pl.BlockSpec(memory_space=pltpu.VMEM),
        scratch_shapes=[
            pltpu.VMEM((rows, cols), jnp.int32),
            pltpu.VMEM((rows, cols), jnp.bfloat16),
            pltpu.VMEM((ROOTS, rows, cols), jnp.bfloat16),
            pltpu.VMEM((ROOTS * cols, cols), jnp.bfloat16),
            pltpu.SemaphoreType.DMA((rows // PIECE,)),
            pltpu.SemaphoreType.DMA((ROOTS * 4, chunks)),
            pltpu.SemaphoreType.DMA((ROOTS * 4, 4)),
            pltpu.SemaphoreType.DMA((rows // 2 // RCHUNK,)),
            pltpu.SemaphoreType.DMA,
            pltpu.SemaphoreType.DMA,
            pltpu.SemaphoreType.DMA,
        ],
        compiler_params=pltpu.CompilerParams(
            collective_id=0, has_side_effects=True, vmem_limit_bytes=48 * 1024 * 1024
        ),
    )(adjacency)


def solution(mesh):
    spec = P("row", "col")
    return jax.shard_map(per_device, mesh=mesh, in_specs=(spec,), out_specs=spec, check_vma=False)
```

time: 279 us -> 98.5 us (0.35)
  the two profiles are of different devices: /device:TPU:1 before, /device:TPU:16 now
where the time goes in v1:
time: 98.5 us; the launch traced here: 98.4 us
  Pallas kernels  96.4 us (98%)
  local copies, waits for them, and re-layouts  2.02 us (2%)
    pallas_call x1, Pallas kernels, per_device(): pl.pallas_call(kernel, name='closure', out_shape=jax.ShapeDtypeStruct((ro...  96.4 us
    unnamed x1, local copies, waits for them, and re-layouts  2.02 us

profile of v1, /device:TPU:16, one launch (start us, length us, event | category | flops | bytes accessed | tf_op | source)
XLA Modules:
  0.0 98.4 jit_solution(407416228310695842)
XLA Ops:
  0.0 96.4 %closure.1 = bf16[2048,1024]{1,0:T(8,128)(2,1)S(1)} custom-call(s32[2048,1024]{1,0:T(8,128)} %adj_ref.1), custom_call_target="tpu_custom_call" | custom-call | tf_op jit(solution)/shard_map/closure/pallas_call | solution.py:245
  96.4 2.0 %copy.3 = bf16[2048,1024]{1,0:T(8,128)(2,1)} copy(bf16[2048,1024]{1,0:T(8,128)(2,1)S(1)} %closure.1) | data formatting | bytes 8388608
